TPU v7x, 32 devices: a whole 2x2x4 slice. The times are simulated.
32 devices in a mesh: dp: 8 (over z, x), seq: 4 (over y, core).
Axes of the slice: x: 2, y: 2, z: 4, core: 2. Of those that a mesh axis runs over, the one named last changes fastest.
Arguments:
- queries: bfloat16 [4096, 2048], P(('dp', 'seq')), may hold values from -6 to 6
- keys: bfloat16 [4096, 2048], P(('dp', 'seq')), may hold values from -6 to 6
- values: bfloat16 [4096, 2048], P(('dp', 'seq')), may hold values from -6 to 6
- q_gain: float32 [2048], replicated, may hold values from 0.25 to 1.75
- k_gain: float32 [2048], replicated, may hold values from 0.25 to 1.75
- out_grad: bfloat16 [4096, 2048], P(('dp', 'seq')), may hold values from -16 to 16
- segments: int32 [8, 512], P('dp'), may hold values from 0 to 3, never falling along the last dimension, each value on 1 to 256 neighbouring positions
- visible: int32 [8, 512], P('dp'), may hold values 0 or 1
Outputs:
- attn_out: bfloat16 [4096, 2048], P(('dp', 'seq'))
- query_grad: bfloat16 [4096, 2048], P(('dp', 'seq'))
- key_grad: bfloat16 [4096, 2048], P(('dp', 'seq'))
- value_grad: bfloat16 [4096, 2048], P(('dp', 'seq'))
- q_gain_grad: float32 [2048], replicated
- k_gain_grad: float32 [2048], replicated
Inputs may be any that keep to these rules, and one draw needn't show every extreme that they name: `segments`: along each packed sequence the clip numbers never fall; each of the 4 clips holds 1 to 256 slots.
All inputs are finite; a program needn't handle non-finite values. No bound on the sum of `visible` on one device may be relied on, other than what follows from the above.
Results may differ from a plain program's by a relative error of at most 0.012.
The roundings to bfloat16 on the way count: a program that leaves them out, or rounds other values in their place, can miss the bound.
Values may be sent and summed in bfloat16 or wider, within the bound.
No kernel may reach another device: no remote copies, remote signals or barrier semaphores. Data moves between devices by JAX's collectives and lax.ppermute only.
A program may use at most 64 MiB of HBM per device.

v0:
```python
import jax
import jax.numpy as jnp
from jax import lax
from jax.sharding import PartitionSpec as P

D_HEAD = 128
epsilon = 1e-06


def normalize(raw_rows, gain_vec):
    raw_f32 = raw_rows.astype(jnp.float32)
    inv_rms = lax.rsqrt(jnp.mean(raw_f32 * raw_f32, axis=-1, keepdims=True) + epsilon)
    return ((raw_f32 * inv_rms * gain_vec).astype(jnp.bfloat16), inv_rms)


def norm_back(raw_rows, inv_rms, gain_vec, grad_norm):
    raw_f32 = raw_rows.astype(jnp.float32)
    grad_f32 = grad_norm.astype(jnp.float32)
    scaled_grad = gain_vec * grad_f32
    mean_term = jnp.mean(scaled_grad * raw_f32, axis=-1, keepdims=True)
    grad_raw = inv_rms * scaled_grad - raw_f32 * inv_rms**3 * mean_term
    return (grad_raw.astype(jnp.bfloat16), jnp.sum(grad_f32 * raw_f32 * inv_rms, axis=0))


def attend(q_norm, k_norm, val_rows, grad_rows, seg_row, vis_row, keep_out):
    seq_rows, feature_count = q_norm.shape
    head_count = feature_count // D_HEAD
    score_scale = D_HEAD ** (-0.5)
    block_rows = 512
    block_count = seq_rows // block_rows
    k_three = k_norm.reshape(seq_rows, head_count, D_HEAD)
    v_three = val_rows.reshape(seq_rows, head_count, D_HEAD)
    positions = jnp.arange(seq_rows, dtype=jnp.int32)
    key_open = vis_row == 1

    def one_block(totals, block_index):
        block_start = block_index * block_rows
        q_block = lax.dynamic_slice_in_dim(q_norm, block_start, block_rows, 0).reshape(
            block_rows, head_count, D_HEAD
        )
        seg_block = lax.dynamic_slice_in_dim(seg_row, block_start, block_rows, 0)
        pos_block = block_start + jnp.arange(block_rows, dtype=jnp.int32)
        allowed = (seg_block[:, None] == seg_row[None, :]) & (
            key_open[None, :] | (pos_block[:, None] == positions[None, :])
        )
        scores = (
            jnp.einsum("shd,thd->hst", q_block, k_three, preferred_element_type=jnp.float32)
            * score_scale
        )
        scores = jnp.where(allowed[None], scores, -1e30)
        row_max = jnp.max(scores, axis=-1, keepdims=True)
        weights = jnp.exp(scores - row_max)
        attn_prob = weights / jnp.sum(weights, axis=-1, keepdims=True)
        prob_half = attn_prob.astype(jnp.bfloat16)
        block_out = jnp.zeros((block_rows, feature_count), jnp.bfloat16)
        if keep_out:
            block_out = (
                jnp.einsum("hst,thd->shd", prob_half, v_three, preferred_element_type=jnp.float32)
                .reshape(block_rows, feature_count)
                .astype(jnp.bfloat16)
            )
        if grad_rows is None:
            return (totals, (block_out, block_out))
        grad_block = lax.dynamic_slice_in_dim(grad_rows, block_start, block_rows, 0).reshape(
            block_rows, head_count, D_HEAD
        )
        dprob = jnp.einsum("shd,thd->hst", grad_block, v_three, preferred_element_type=jnp.float32)
        value_add = jnp.einsum(
            "hst,shd->thd", prob_half, grad_block, preferred_element_type=jnp.float32
        )
        row_dot = jnp.sum(attn_prob * dprob, axis=-1, keepdims=True)
        score_grad = (attn_prob * (dprob - row_dot) * score_scale).astype(jnp.bfloat16)
        q_grad = (
            jnp.einsum("hst,thd->shd", score_grad, k_three, preferred_element_type=jnp.float32)
            .reshape(block_rows, feature_count)
            .astype(jnp.bfloat16)
        )
        key_add = jnp.einsum(
            "hst,shd->thd", score_grad, q_block, preferred_element_type=jnp.float32
        )
        return ((totals[0] + key_add, totals[1] + value_add), (block_out, q_grad))

    empty = jnp.zeros((seq_rows, head_count, D_HEAD), jnp.float32)
    totals, stacked = lax.scan(one_block, (empty, empty), jnp.arange(block_count, dtype=jnp.int32))
    attn_out = stacked[0].reshape(seq_rows, feature_count)
    if grad_rows is None:
        return attn_out
    q_grad = stacked[1].reshape(seq_rows, feature_count)
    k_grad = totals[0].reshape(seq_rows, feature_count).astype(jnp.bfloat16)
    v_grad = totals[1].reshape(seq_rows, feature_count).astype(jnp.bfloat16)
    return (attn_out, q_grad, k_grad, v_grad)


def per_device(queries, keys, values, q_gain, k_gain, out_grad, segments, visible):
    q_norm, q_inv = normalize(queries, q_gain)
    k_norm, k_inv = normalize(keys, k_gain)
    seg_row = segments[0]
    vis_row = visible[0]
    query_heads, key_heads, value_heads = (
        lax.all_to_all(q_norm, "seq", split_axis=1, concat_axis=0, tiled=True),
        lax.all_to_all(k_norm, "seq", split_axis=1, concat_axis=0, tiled=True),
        lax.all_to_all(values, "seq", split_axis=1, concat_axis=0, tiled=True),
    )
    out_part = attend(query_heads, key_heads, value_heads, None, seg_row, vis_row, True)
    attn_out = lax.all_to_all(out_part, "seq", split_axis=0, concat_axis=1, tiled=True)
    grad_heads = lax.all_to_all(out_grad, "seq", split_axis=1, concat_axis=0, tiled=True)
    unused_out, q_part, k_part, v_part = attend(
        query_heads, key_heads, value_heads, grad_heads, seg_row, vis_row, False
    )
    q_grad, k_grad, value_grad = (
        lax.all_to_all(q_part, "seq", split_axis=0, concat_axis=1, tiled=True),
        lax.all_to_all(k_part, "seq", split_axis=0, concat_axis=1, tiled=True),
        lax.all_to_all(v_part, "seq", split_axis=0, concat_axis=1, tiled=True),
    )
    query_grad, q_gain_part = norm_back(queries, q_inv, q_gain, q_grad)
    key_grad, k_gain_part = norm_back(keys, k_inv, k_gain, k_grad)
    q_gain_grad, k_gain_grad = lax.psum((q_gain_part, k_gain_part), ("dp", "seq"))
    return (attn_out, query_grad, key_grad, value_grad, q_gain_grad, k_gain_grad)


def solution(mesh):
    return jax.shard_map(
        per_device,
        mesh=mesh,
        in_specs=(
            P(("dp", "seq"), None),
            P(("dp", "seq"), None),
            P(("dp", "seq"), None),
            P(),
            P(),
            P(("dp", "seq"), None),
            P("dp", None),
            P("dp", None),
        ),
        out_specs=(
            P(("dp", "seq"), None),
            P(("dp", "seq"), None),
            P(("dp", "seq"), None),
            P(("dp", "seq"), None),
            P(),
            P(),
        ),
        check_vma=False,
    )
```

profile of v0, /device:TPU:0, one launch (start us, length us, event | category | flops | bytes accessed | tf_op | source)
XLA Modules:
  0.0 164.4 jit_solution(12461290162924541765)
XLA Ops:
  0.6 0.0 copy-start.1
  0.6 0.0 copy-start.5
  0.7 0.0 copy-start.2
  0.7 1.3 fusion.31
  2.0 1.2 fusion.33
  3.2 0.0 copy-start.3
  3.2 0.8 copy.112
  4.1 4.3 %all-to-all-start = ((bf16[128,4,512]{2,0,1:T(8,128)(2,1)}), bf16[128,4,512]{2,0,1:T(8,128)(2,1)S(1)}, u32[]{:S(2)}, u32[]{:S(2)}) async-start(bf16[128,4,512]{2,0,1:T(8,128)(2,1)} %bitcast.48), calls=%async_computation | async-start | bytes 1048576 | tf_op jit(solution)/shard_map/all_to_all | solution.py:100
  8.4 1.3 fusion.40
  9.6 0.0 copy-done.5
  9.6 0.2 fusion.42
  9.8 0.8 copy.111
  10.7 6.5 %all-to-all-done = bf16[128,4,512]{2,0,1:T(8,128)(2,1)S(1)} async-done(((bf16[128,4,512]{2,0,1:T(8,128)(2,1)}), bf16[128,4,512]{2,0,1:T(8,128)(2,1)S(1)}, u32[]{:S(2)}, u32[]{:S(2)}) %all-to-all-start) | async-done | bytes 524320 | tf_op jit(solution)/shard_map/all_to_all | solution.py:100
  17.2 3.5 %all-to-all-start.1 = ((bf16[128,4,512]{2,0,1:T(8,128)(2,1)}), bf16[128,4,512]{2,0,1:T(8,128)(2,1)S(1)}, u32[]{:S(2)}, u32[]{:S(2)}) async-start(bf16[128,4,512]{2,0,1:T(8,128)(2,1)} %bitcast.47), calls=%async_computation.1 | async-start | bytes 1048576 | tf_op jit(solution)/shard_map/all_to_all | solution.py:101
  20.7 0.8 copy.110
  21.5 7.9 %all-to-all-done.1 = bf16[128,4,512]{2,0,1:T(8,128)(2,1)S(1)} async-done(((bf16[128,4,512]{2,0,1:T(8,128)(2,1)}), bf16[128,4,512]{2,0,1:T(8,128)(2,1)S(1)}, u32[]{:S(2)}, u32[]{:S(2)}) %all-to-all-start.1) | async-done | bytes 524320 | tf_op jit(solution)/shard_map/all_to_all | solution.py:101
  29.4 3.5 %all-to-all-start.2 = ((bf16[128,4,512]{2,0,1:T(8,128)(2,1)}), bf16[128,4,512]{2,0,1:T(8,128)(2,1)S(1)}, u32[]{:S(2)}, u32[]{:S(2)}) async-start(bf16[128,4,512]{2,0,1:T(8,128)(2,1)} %bitcast.46), calls=%async_computation.2 | async-start | bytes 1048576 | tf_op jit(solution)/shard_map/all_to_all | solution.py:102
  32.9 0.8 copy.109
  33.8 7.9 %all-to-all-done.2 = bf16[128,4,512]{2,0,1:T(8,128)(2,1)S(1)} async-done(((bf16[128,4,512]{2,0,1:T(8,128)(2,1)}), bf16[128,4,512]{2,0,1:T(8,128)(2,1)S(1)}, u32[]{:S(2)}, u32[]{:S(2)}) %all-to-all-start.2) | async-done | bytes 524320 | tf_op jit(solution)/shard_map/all_to_all | solution.py:102
  41.7 3.5 %all-to-all-start.4 = ((bf16[128,4,512]{2,0,1:T(8,128)(2,1)}), bf16[128,4,512]{2,0,1:T(8,128)(2,1)S(1)}, u32[]{:S(2)}, u32[]{:S(2)}) async-start(bf16[128,4,512]{2,0,1:T(8,128)(2,1)} %bitcast.45), calls=%async_computation.4 | async-start | bytes 1048576 | tf_op jit(solution)/shard_map/all_to_all | solution.py:106
  45.2 0.3 fusion.52
  45.5 0.1 reshape.189
  45.6 1.1 copy.79
  46.7 0.1 reshape.190
  46.9 0.3 copy.75
  47.2 0.1 reshape.191
  47.3 6.6 %all-to-all-done.4 = bf16[128,4,512]{2,0,1:T(8,128)(2,1)S(1)} async-done(((bf16[128,4,512]{2,0,1:T(8,128)(2,1)}), bf16[128,4,512]{2,0,1:T(8,128)(2,1)S(1)}, u32[]{:S(2)}, u32[]{:S(2)}) %all-to-all-start.4) | async-done | bytes 524320 | tf_op jit(solution)/shard_map/all_to_all | solution.py:106
  53.9 0.1 reshape.192
  54.1 4.7 %fusion.66 = (f32[4,512]{1,0:T(4,128)S(1)}, f32[4,512,512]{1,2,0:T(8,128)}) fusion(pred[512,512]{0,1:T(8,128)(4,1)S(1)} %fusion.52, bf16[512,4,128]{0,2,1:T(8,128)(2,1)} %copy.79, bf16[512,4,128]{0,2,1:T(8,128)(2,1)S(1)} %copy.75), kind=kOutput, calls=%fused_computation.80 | convolution fusion | flops 272630272 | bytes 5513216 | tf_op jit(solution)/shard_map/while/body/eval_jaxpr/sub | solution.py:52
  58.7 2.9 %fusion.30 = bf16[512,4,128]{2,0,1:T(8,128)(2,1)S(1)} fusion(bf16[512,4,128]{2,1,0:T(4,128)(2,1)S(1)} %reshape.192, f32[4,512,512]{1,2,0:T(8,128)} %get-tuple-element.92, f32[4,512]{1,0:T(4,128)S(1)} %get-tuple-element.91), kind=kOutput, calls=%fused_computation.33 | convolution fusion | flops 270794752 | bytes 5251072 | tf_op jit(solution)/shard_map/while/body/eval_jaxpr/hst,shd->thd/dot_general | solution.py:68
  61.7 0.4 copy.84
  62.1 1.0 convert_element_type.117
  63.1 3.5 %all-to-all-start.7 = ((bf16[4,128,512]{2,1,0:T(8,128)(2,1)}), bf16[4,128,512]{2,1,0:T(8,128)(2,1)S(1)}, u32[]{:S(2)}, u32[]{:S(2)}) async-start(bf16[4,128,512]{2,1,0:T(8,128)(2,1)} %convert_element_type.117), calls=%async_computation.7 | async-start | bytes 1048576 | tf_op jit(solution)/shard_map/all_to_all | solution.py:113
  66.5 3.1 %fusion.29 = bf16[512,4,128]{2,0,1:T(8,128)(2,1)S(1)} fusion(bf16[512,4,128]{2,1,0:T(4,128)(2,1)S(1)} %reshape.191, f32[4,512,512]{1,2,0:T(8,128)} %get-tuple-element.92, f32[4,512]{1,0:T(4,128)S(1)} %get-tuple-element.91), kind=kOutput, calls=%fused_computation.32 | convolution fusion | flops 270794752 | bytes 5251072 | tf_op jit(solution)/shard_map/while/body/eval_jaxpr/hst,thd->shd/dot_general | solution.py:58
  69.6 0.4 copy.70
  70.1 1.0 convert_element_type.99
  71.1 4.3 %all-to-all-done.7 = bf16[4,128,512]{2,1,0:T(8,128)(2,1)S(1)} async-done(((bf16[4,128,512]{2,1,0:T(8,128)(2,1)}), bf16[4,128,512]{2,1,0:T(8,128)(2,1)S(1)}, u32[]{:S(2)}, u32[]{:S(2)}) %all-to-all-start.7) | async-done | bytes 524320 | tf_op jit(solution)/shard_map/all_to_all | solution.py:113
  75.3 3.5 %all-to-all-start.3 = ((bf16[4,128,512]{2,1,0:T(8,128)(2,1)}), bf16[4,128,512]{2,1,0:T(8,128)(2,1)S(1)}, u32[]{:S(2)}, u32[]{:S(2)}) async-start(bf16[4,128,512]{2,1,0:T(8,128)(2,1)} %convert_element_type.99), calls=%async_computation.3 | async-start | bytes 1048576 | tf_op jit(solution)/shard_map/all_to_all | solution.py:105
  78.8 2.7 %fusion.54 = f32[4,512,512]{1,2,0:T(8,128)} fusion(bf16[512,4,128]{2,1,0:T(4,128)(2,1)S(1)} %reshape.192, bf16[512,4,128]{2,1,0:T(4,128)(2,1)S(1)} %reshape.191), kind=kOutput, calls=%fused_computation.62 | convolution fusion | flops 268435456 | bytes 5242880 | tf_op jit(solution)/shard_map/while/body/eval_jaxpr/shd,thd->hst/dot_general | solution.py:67
  81.5 7.6 %fusion.23 = bf16[512,4,128]{0,2,1:T(8,128)(2,1)S(1)} fusion(bf16[512,4,128]{0,2,1:T(8,128)(2,1)} %copy.79, f32[4,512,512]{1,2,0:T(8,128)} %fusion.54, f32[4,512,512]{1,2,0:T(8,128)} %get-tuple-element.92, f32[4,512]{1,0:T(4,128)S(1)} %get-tuple-element.91), kind=kOutput, calls=%fused_computation.30 | convolution fusion | flops 276040192 | bytes 9445376 | tf_op jit(solution)/shard_map/while/body/eval_jaxpr/hst,shd->thd/dot_general | solution.py:78
  89.1 0.1 convert_element_type.110
  89.2 0.9 copy.81
  90.1 0.0 all-to-all-done.3
  90.1 3.5 %all-to-all-start.6 = ((bf16[4,128,512]{1,2,0:T(8,128)(2,1)}), bf16[4,128,512]{1,2,0:T(8,128)(2,1)S(1)}, u32[]{:S(2)}, u32[]{:S(2)}) async-start(bf16[4,128,512]{1,2,0:T(8,128)(2,1)} %copy.81), calls=%async_computation.6 | async-start | bytes 1048576 | tf_op jit(solution)/shard_map/all_to_all | solution.py:112
  93.6 8.5 %fusion.26 = bf16[512,4,128]{0,2,1:T(8,128)(2,1)} fusion(bf16[512,4,128]{0,2,1:T(8,128)(2,1)S(1)} %copy.75, f32[4,512,512]{1,2,0:T(8,128)} %fusion.54, f32[4,512,512]{1,2,0:T(8,128)} %get-tuple-element.92, f32[4,512]{1,0:T(4,128)S(1)} %get-tuple-element.91), kind=kOutput, calls=%fused_computation.31 | convolution fusion | flops 276040192 | bytes 9445376 | tf_op jit(solution)/shard_map/while/body/eval_jaxpr/hst,thd->shd/dot_general | solution.py:74
  102.1 1.2 convert_element_type.103
  103.3 0.9 copy.77
  104.2 0.0 all-to-all-done.6
  104.2 4.3 %all-to-all-start.5 = ((bf16[4,128,512]{1,2,0:T(8,128)(2,1)}), bf16[4,128,512]{1,2,0:T(8,128)(2,1)}, u32[]{:S(2)}, u32[]{:S(2)}) async-start(bf16[4,128,512]{1,2,0:T(8,128)(2,1)} %copy.77), calls=%async_computation.5 | async-start | bytes 1048576 | tf_op jit(solution)/shard_map/all_to_all | solution.py:111
  108.5 0.3 copy.85
  108.8 1.0 copy.89
  109.8 0.3 copy.71
  110.0 0.0 copy-start
  110.1 0.0 copy-start.4
  110.1 1.0 copy.88
  111.1 0.1 convert_element_type.121
  111.2 0.3 copy.82
  111.5 5.8 %all-to-all-done.5 = bf16[4,128,512]{1,2,0:T(8,128)(2,1)} async-done(((bf16[4,128,512]{1,2,0:T(8,128)(2,1)}), bf16[4,128,512]{1,2,0:T(8,128)(2,1)}, u32[]{:S(2)}, u32[]{:S(2)}) %all-to-all-start.5) | async-done | bytes 524320 | tf_op jit(solution)/shard_map/all_to_all | solution.py:111
  117.3 2.1 %convert_element_type.120 = f32[4,128,512]{1,2,0:T(8,128)} convert(bf16[4,128,512]{1,2,0:T(8,128)(2,1)} %all-to-all-done.5) | non-fusion elementwise | flops 262144 | bytes 1572864 | tf_op jit(solution)/shard_map/convert_element_type | solution.py:18
  119.4 1.6 copy.78
  121.0 0.6 fusion.39
  121.7 40.3 %all-reduce = (f32[2048]{0:T(1024)}, f32[2048]{0:T(1024)}) all-reduce(f32[2048]{0:T(1024)S(1)} %get-tuple-element.71, f32[2048]{0:T(1024)S(1)} %get-tuple-element.94), channel_id=1, replica_groups=mesh['dp'=8,'seq'=4] {'dp','seq'}, use_global_device_ids=true, to_apply=%region_8.9 | all-reduce | flops 4096 | bytes 32768 | tf_op jit(solution)/shard_map/psum | solution.py:117
  162.0 1.2 fusion.36
  163.2 1.2 fusion.45
  (14 shorter events, 0.1 us)
Async XLA Ops:
  0.6 9.0 %copy-start.1 = (bf16[128,2048]{1,0:T(8,128)(2,1)S(1)}, bf16[128,2048]{1,0:T(8,128)(2,1)}, u32[]{:S(2)}) copy-start(bf16[128,2048]{1,0:T(8,128)(2,1)} %param.9) | copy-start | bytes 1572868
  0.6 9.0 %copy-start.5 = (f32[2048]{0:T(1024)S(1)}, f32[2048]{0:T(1024)}, u32[]{:S(2)}) copy-start(f32[2048]{0:T(1024)} %param.12) | copy-start | bytes 24580
  0.7 20.0 %copy-start.2 = (bf16[128,2048]{1,0:T(8,128)(2,1)S(1)}, bf16[128,2048]{1,0:T(8,128)(2,1)}, u32[]{:S(2)}) copy-start(bf16[128,2048]{1,0:T(8,128)(2,1)} %param.10) | copy-start | bytes 1572868
  3.2 29.7 %copy-start.3 = (bf16[128,2048]{1,0:T(8,128)(2,1)S(1)}, bf16[128,2048]{1,0:T(8,128)(2,1)}, u32[]{:S(2)}) copy-start(bf16[128,2048]{1,0:T(8,128)(2,1)} %param.13) | copy-start | bytes 1572868
  4.1 13.1 %all-to-all-start = ((bf16[128,4,512]{2,0,1:T(8,128)(2,1)}), bf16[128,4,512]{2,0,1:T(8,128)(2,1)S(1)}, u32[]{:S(2)}, u32[]{:S(2)}) async-start(bf16[128,4,512]{2,0,1:T(8,128)(2,1)} %bitcast.48), calls=%async_computation | async-start | bytes 1048576 | tf_op jit(solution)/shard_map/all_to_all | solution.py:100
  8.3 36.8 %copy-start.7 = (s32[1,512]{1,0:T(1,128)S(1)}, s32[1,512]{1,0:T(1,128)}, u32[]{:S(2)}) copy-start(s32[1,512]{1,0:T(1,128)} %param.15) | copy-start | bytes 6148
  8.3 36.8 %copy-start.6 = (s32[1,512]{1,0:T(1,128)S(1)}, s32[1,512]{1,0:T(1,128)}, u32[]{:S(2)}) copy-start(s32[1,512]{1,0:T(1,128)} %param.14) | copy-start | bytes 6148
  17.2 12.3 %all-to-all-start.1 = ((bf16[128,4,512]{2,0,1:T(8,128)(2,1)}), bf16[128,4,512]{2,0,1:T(8,128)(2,1)S(1)}, u32[]{:S(2)}, u32[]{:S(2)}) async-start(bf16[128,4,512]{2,0,1:T(8,128)(2,1)} %bitcast.47), calls=%async_computation.1 | async-start | bytes 1048576 | tf_op jit(solution)/shard_map/all_to_all | solution.py:101
  29.4 12.3 %all-to-all-start.2 = ((bf16[128,4,512]{2,0,1:T(8,128)(2,1)}), bf16[128,4,512]{2,0,1:T(8,128)(2,1)S(1)}, u32[]{:S(2)}, u32[]{:S(2)}) async-start(bf16[128,4,512]{2,0,1:T(8,128)(2,1)} %bitcast.46), calls=%async_computation.2 | async-start | bytes 1048576 | tf_op jit(solution)/shard_map/all_to_all | solution.py:102
  41.7 12.3 %all-to-all-start.4 = ((bf16[128,4,512]{2,0,1:T(8,128)(2,1)}), bf16[128,4,512]{2,0,1:T(8,128)(2,1)S(1)}, u32[]{:S(2)}, u32[]{:S(2)}) async-start(bf16[128,4,512]{2,0,1:T(8,128)(2,1)} %bitcast.45), calls=%async_computation.4 | async-start | bytes 1048576 | tf_op jit(solution)/shard_map/all_to_all | solution.py:106
  63.1 12.3 %all-to-all-start.7 = ((bf16[4,128,512]{2,1,0:T(8,128)(2,1)}), bf16[4,128,512]{2,1,0:T(8,128)(2,1)S(1)}, u32[]{:S(2)}, u32[]{:S(2)}) async-start(bf16[4,128,512]{2,1,0:T(8,128)(2,1)} %convert_element_type.117), calls=%async_computation.7 | async-start | bytes 1048576 | tf_op jit(solution)/shard_map/all_to_all | solution.py:113
  75.3 14.8 %all-to-all-start.3 = ((bf16[4,128,512]{2,1,0:T(8,128)(2,1)}), bf16[4,128,512]{2,1,0:T(8,128)(2,1)S(1)}, u32[]{:S(2)}, u32[]{:S(2)}) async-start(bf16[4,128,512]{2,1,0:T(8,128)(2,1)} %convert_element_type.99), calls=%async_computation.3 | async-start | bytes 1048576 | tf_op jit(solution)/shard_map/all_to_all | solution.py:105
  90.1 14.0 %all-to-all-start.6 = ((bf16[4,128,512]{1,2,0:T(8,128)(2,1)}), bf16[4,128,512]{1,2,0:T(8,128)(2,1)S(1)}, u32[]{:S(2)}, u32[]{:S(2)}) async-start(bf16[4,128,512]{1,2,0:T(8,128)(2,1)} %copy.81), calls=%async_computation.6 | async-start | bytes 1048576 | tf_op jit(solution)/shard_map/all_to_all | solution.py:112
  104.2 13.2 %all-to-all-start.5 = ((bf16[4,128,512]{1,2,0:T(8,128)(2,1)}), bf16[4,128,512]{1,2,0:T(8,128)(2,1)}, u32[]{:S(2)}, u32[]{:S(2)}) async-start(bf16[4,128,512]{1,2,0:T(8,128)(2,1)} %copy.77), calls=%async_computation.5 | async-start | bytes 1048576 | tf_op jit(solution)/shard_map/all_to_all | solution.py:111
  110.0 10.9 %copy-start = (bf16[128,2048]{1,0:T(8,128)(2,1)S(1)}, bf16[128,2048]{1,0:T(8,128)(2,1)}, u32[]{:S(2)}) copy-start(bf16[128,2048]{1,0:T(8,128)(2,1)} %param.8) | copy-start | bytes 1572868
  110.1 10.9 %copy-start.4 = (f32[2048]{0:T(1024)S(1)}, f32[2048]{0:T(1024)}, u32[]{:S(2)}) copy-start(f32[2048]{0:T(1024)} %param.11) | copy-start | bytes 24580
where the time goes:
time: 165 us; the launch traced here: 164 us
  blocking collectives  40.3 us (24%)
  waiting for transfers between devices  39.1 us (24%)
  matrix products  29.5 us (18%)
  starting transfers between devices  29.4 us (18%)
  local copies, waits for them, and re-layouts  15.6 us (9%)
  other arithmetic  9.54 us (6%)
    psum x1, blocking collectives, per_device(): lax.psum((q_gain_part, k_gain_part), ('dp', 'seq'))  40.3 us
    dot_general x1, matrix products, one_block(): jnp.einsum('hst,thd->shd', score_grad, k_three, preferred_element_type=jn...  8.53 us
    all_to_all x1, waiting for transfers between devices, per_device(): lax.all_to_all(k_norm, 'seq', split_axis=1, concat_axis=0, tiled=True)  7.93 us
    all_to_all x1, waiting for transfers between devices, per_device(): lax.all_to_all(values, 'seq', split_axis=1, concat_axis=0, tiled=True)  7.93 us
    dot_general x1, matrix products, one_block(): jnp.einsum('hst,shd->thd', score_grad, q_block, preferred_element_type=jn...  7.62 us
    all_to_all x1, waiting for transfers between devices, per_device(): lax.all_to_all(out_grad, 'seq', split_axis=1, concat_axis=0, tiled=True)  6.63 us
    all_to_all x1, waiting for transfers between devices, per_device(): lax.all_to_all(q_norm, 'seq', split_axis=1, concat_axis=0, tiled=True)  6.49 us
    all_to_all x1, waiting for transfers between devices, per_device(): lax.all_to_all(q_part, 'seq', split_axis=0, concat_axis=1, tiled=True)  5.84 us
  transfers between devices with their start and end apart: 8, of which 6 were waited for; matrix products, arithmetic and copies ran while one was open for 22% of the time, Pallas kernels for 0%

commit v1 on v0

--- a/solution.py
+++ b/solution.py
@@ -114,7 +114,10 @@
     )
     query_grad, q_gain_part = norm_back(queries, q_inv, q_gain, q_grad)
     key_grad, k_gain_part = norm_back(keys, k_inv, k_gain, k_grad)
-    q_gain_grad, k_gain_grad = lax.psum((q_gain_part, k_gain_part), ("dp", "seq"))
+    tell_units = lambda mesh_ax, w_in, ax_name: lax.psum(
+        lax.psum(w_in, axis_name=ax_name), axis_name=mesh_ax
+    )
+    q_gain_grad, k_gain_grad = tell_units("seq", (q_gain_part, k_gain_part), "dp")
     return (attn_out, query_grad, key_grad, value_grad, q_gain_grad, k_gain_grad)
 
 

time: 165 us -> 174 us (1.055)
  blocking collectives: 40.3 us -> 48.8 us
    psum x1 -> x2, blocking collectives: 40.3 us -> 48.8 us  [the longest x1 38 us: per_device(): lax.psum(w_in, axis_name=ax_name)]
  transfers between devices with their start and end apart: 8 -> 8, of which waited for: 6 -> 6; matrix products, arithmetic and copies ran while one was open for 22% -> 20% of each run, Pallas kernels for 0% -> 0%
where the time goes in v1:
time: 174 us; the launch traced here: 173 us
  blocking collectives  48.8 us (28%)
  waiting for transfers between devices  39.1 us (22%)
  matrix products  29.5 us (17%)
  starting transfers between devices  29.4 us (17%)
  local copies, waits for them, and re-layouts  15.6 us (9%)
  other arithmetic  9.53 us (5%)
    psum x1, blocking collectives, per_device(): lax.psum(w_in, axis_name=ax_name)  38 us
    psum x1, blocking collectives, per_device(): lax.psum(lax.psum(w_in, axis_name=ax_name), axis_name=mesh_ax)  10.7 us
    dot_general x1, matrix products, one_block(): jnp.einsum('hst,thd->shd', score_grad, k_three, preferred_element_type=jn...  8.53 us
    all_to_all x1, waiting for transfers between devices, per_device(): lax.all_to_all(k_norm, 'seq', split_axis=1, concat_axis=0, tiled=True)  7.93 us
    all_to_all x1, waiting for transfers between devices, per_device(): lax.all_to_all(values, 'seq', split_axis=1, concat_axis=0, tiled=True)  7.93 us
    dot_general x1, matrix products, one_block(): jnp.einsum('hst,shd->thd', score_grad, q_block, preferred_element_type=jn...  7.62 us
    all_to_all x1, waiting for transfers between devices, per_device(): lax.all_to_all(out_grad, 'seq', split_axis=1, concat_axis=0, tiled=True)  6.63 us
    all_to_all x1, waiting for transfers between devices, per_device(): lax.all_to_all(q_norm, 'seq', split_axis=1, concat_axis=0, tiled=True)  6.49 us
  transfers between devices with their start and end apart: 8, of which 6 were waited for; matrix products, arithmetic and copies ran while one was open for 20% of the time, Pallas kernels for 0%

profile of v1, /device:TPU:0, one launch (start us, length us, event | category | flops | bytes accessed | tf_op | source)
XLA Modules:
  0.0 172.9 jit_solution(5972317618414314924)
XLA Ops:
  0.6 0.0 copy-start.1
  0.6 0.0 copy-start.5
  0.7 0.0 copy-start.2
  0.7 1.3 fusion.31
  2.0 1.2 fusion.33
  3.2 0.0 copy-start.3
  3.2 0.8 copy.112
  4.1 4.3 %all-to-all-start = ((bf16[128,4,512]{2,0,1:T(8,128)(2,1)}), bf16[128,4,512]{2,0,1:T(8,128)(2,1)S(1)}, u32[]{:S(2)}, u32[]{:S(2)}) async-start(bf16[128,4,512]{2,0,1:T(8,128)(2,1)} %bitcast.48), calls=%async_computation | async-start | bytes 1048576 | tf_op jit(solution)/shard_map/all_to_all | solution.py:100
  8.4 1.3 fusion.40
  9.6 0.2 fusion.42
  9.8 0.8 copy.111
  10.7 6.5 %all-to-all-done = bf16[128,4,512]{2,0,1:T(8,128)(2,1)S(1)} async-done(((bf16[128,4,512]{2,0,1:T(8,128)(2,1)}), bf16[128,4,512]{2,0,1:T(8,128)(2,1)S(1)}, u32[]{:S(2)}, u32[]{:S(2)}) %all-to-all-start) | async-done | bytes 524320 | tf_op jit(solution)/shard_map/all_to_all | solution.py:100
  17.2 3.5 %all-to-all-start.1 = ((bf16[128,4,512]{2,0,1:T(8,128)(2,1)}), bf16[128,4,512]{2,0,1:T(8,128)(2,1)S(1)}, u32[]{:S(2)}, u32[]{:S(2)}) async-start(bf16[128,4,512]{2,0,1:T(8,128)(2,1)} %bitcast.47), calls=%async_computation.1 | async-start | bytes 1048576 | tf_op jit(solution)/shard_map/all_to_all | solution.py:101
  20.7 0.8 copy.110
  21.5 7.9 %all-to-all-done.1 = bf16[128,4,512]{2,0,1:T(8,128)(2,1)S(1)} async-done(((bf16[128,4,512]{2,0,1:T(8,128)(2,1)}), bf16[128,4,512]{2,0,1:T(8,128)(2,1)S(1)}, u32[]{:S(2)}, u32[]{:S(2)}) %all-to-all-start.1) | async-done | bytes 524320 | tf_op jit(solution)/shard_map/all_to_all | solution.py:101
  29.4 3.5 %all-to-all-start.2 = ((bf16[128,4,512]{2,0,1:T(8,128)(2,1)}), bf16[128,4,512]{2,0,1:T(8,128)(2,1)S(1)}, u32[]{:S(2)}, u32[]{:S(2)}) async-start(bf16[128,4,512]{2,0,1:T(8,128)(2,1)} %bitcast.46), calls=%async_computation.2 | async-start | bytes 1048576 | tf_op jit(solution)/shard_map/all_to_all | solution.py:102
  32.9 0.8 copy.109
  33.8 7.9 %all-to-all-done.2 = bf16[128,4,512]{2,0,1:T(8,128)(2,1)S(1)} async-done(((bf16[128,4,512]{2,0,1:T(8,128)(2,1)}), bf16[128,4,512]{2,0,1:T(8,128)(2,1)S(1)}, u32[]{:S(2)}, u32[]{:S(2)}) %all-to-all-start.2) | async-done | bytes 524320 | tf_op jit(solution)/shard_map/all_to_all | solution.py:102
  41.7 3.5 %all-to-all-start.4 = ((bf16[128,4,512]{2,0,1:T(8,128)(2,1)}), bf16[128,4,512]{2,0,1:T(8,128)(2,1)S(1)}, u32[]{:S(2)}, u32[]{:S(2)}) async-start(bf16[128,4,512]{2,0,1:T(8,128)(2,1)} %bitcast.45), calls=%async_computation.4 | async-start | bytes 1048576 | tf_op jit(solution)/shard_map/all_to_all | solution.py:106
  45.2 0.3 fusion.52
  45.5 0.1 reshape.189
  45.6 1.1 copy.79
  46.7 0.1 reshape.190
  46.9 0.3 copy.75
  47.2 0.1 reshape.191
  47.3 6.6 %all-to-all-done.4 = bf16[128,4,512]{2,0,1:T(8,128)(2,1)S(1)} async-done(((bf16[128,4,512]{2,0,1:T(8,128)(2,1)}), bf16[128,4,512]{2,0,1:T(8,128)(2,1)S(1)}, u32[]{:S(2)}, u32[]{:S(2)}) %all-to-all-start.4) | async-done | bytes 524320 | tf_op jit(solution)/shard_map/all_to_all | solution.py:106
  53.9 0.1 reshape.192
  54.1 4.7 %fusion.66 = (f32[4,512]{1,0:T(4,128)S(1)}, f32[4,512,512]{1,2,0:T(8,128)}) fusion(pred[512,512]{0,1:T(8,128)(4,1)S(1)} %fusion.52, bf16[512,4,128]{0,2,1:T(8,128)(2,1)} %copy.79, bf16[512,4,128]{0,2,1:T(8,128)(2,1)S(1)} %copy.75), kind=kOutput, calls=%fused_computation.80 | convolution fusion | flops 272630272 | bytes 5513216 | tf_op jit(solution)/shard_map/while/body/eval_jaxpr/sub | solution.py:52
  58.7 2.9 %fusion.30 = bf16[512,4,128]{2,0,1:T(8,128)(2,1)S(1)} fusion(bf16[512,4,128]{2,1,0:T(4,128)(2,1)S(1)} %reshape.192, f32[4,512,512]{1,2,0:T(8,128)} %get-tuple-element.94, f32[4,512]{1,0:T(4,128)S(1)} %get-tuple-element.93), kind=kOutput, calls=%fused_computation.33 | convolution fusion | flops 270794752 | bytes 5251072 | tf_op jit(solution)/shard_map/while/body/eval_jaxpr/hst,shd->thd/dot_general | solution.py:68
  61.7 0.4 copy.84
  62.1 1.0 convert_element_type.117
  63.1 3.5 %all-to-all-start.7 = ((bf16[4,128,512]{2,1,0:T(8,128)(2,1)}), bf16[4,128,512]{2,1,0:T(8,128)(2,1)S(1)}, u32[]{:S(2)}, u32[]{:S(2)}) async-start(bf16[4,128,512]{2,1,0:T(8,128)(2,1)} %convert_element_type.117), calls=%async_computation.7 | async-start | bytes 1048576 | tf_op jit(solution)/shard_map/all_to_all | solution.py:113
  66.5 3.1 %fusion.29 = bf16[512,4,128]{2,0,1:T(8,128)(2,1)S(1)} fusion(bf16[512,4,128]{2,1,0:T(4,128)(2,1)S(1)} %reshape.191, f32[4,512,512]{1,2,0:T(8,128)} %get-tuple-element.94, f32[4,512]{1,0:T(4,128)S(1)} %get-tuple-element.93), kind=kOutput, calls=%fused_computation.32 | convolution fusion | flops 270794752 | bytes 5251072 | tf_op jit(solution)/shard_map/while/body/eval_jaxpr/hst,thd->shd/dot_general | solution.py:58
  69.6 0.4 copy.70
  70.1 1.0 convert_element_type.99
  71.1 4.3 %all-to-all-done.7 = bf16[4,128,512]{2,1,0:T(8,128)(2,1)S(1)} async-done(((bf16[4,128,512]{2,1,0:T(8,128)(2,1)}), bf16[4,128,512]{2,1,0:T(8,128)(2,1)S(1)}, u32[]{:S(2)}, u32[]{:S(2)}) %all-to-all-start.7) | async-done | bytes 524320 | tf_op jit(solution)/shard_map/all_to_all | solution.py:113
  75.3 3.5 %all-to-all-start.3 = ((bf16[4,128,512]{2,1,0:T(8,128)(2,1)}), bf16[4,128,512]{2,1,0:T(8,128)(2,1)S(1)}, u32[]{:S(2)}, u32[]{:S(2)}) async-start(bf16[4,128,512]{2,1,0:T(8,128)(2,1)} %convert_element_type.99), calls=%async_computation.3 | async-start | bytes 1048576 | tf_op jit(solution)/shard_map/all_to_all | solution.py:105
  78.8 2.7 %fusion.54 = f32[4,512,512]{1,2,0:T(8,128)} fusion(bf16[512,4,128]{2,1,0:T(4,128)(2,1)S(1)} %reshape.192, bf16[512,4,128]{2,1,0:T(4,128)(2,1)S(1)} %reshape.191), kind=kOutput, calls=%fused_computation.62 | convolution fusion | flops 268435456 | bytes 5242880 | tf_op jit(solution)/shard_map/while/body/eval_jaxpr/shd,thd->hst/dot_general | solution.py:67
  81.5 7.6 %fusion.23 = bf16[512,4,128]{0,2,1:T(8,128)(2,1)S(1)} fusion(bf16[512,4,128]{0,2,1:T(8,128)(2,1)} %copy.79, f32[4,512,512]{1,2,0:T(8,128)} %fusion.54, f32[4,512,512]{1,2,0:T(8,128)} %get-tuple-element.94, f32[4,512]{1,0:T(4,128)S(1)} %get-tuple-element.93), kind=kOutput, calls=%fused_computation.30 | convolution fusion | flops 276040192 | bytes 9445376 | tf_op jit(solution)/shard_map/while/body/eval_jaxpr/hst,shd->thd/dot_general | solution.py:78
  89.1 0.1 convert_element_type.110
  89.2 0.9 copy.81
  90.1 0.0 all-to-all-done.3
  90.1 3.5 %all-to-all-start.6 = ((bf16[4,128,512]{1,2,0:T(8,128)(2,1)}), bf16[4,128,512]{1,2,0:T(8,128)(2,1)S(1)}, u32[]{:S(2)}, u32[]{:S(2)}) async-start(bf16[4,128,512]{1,2,0:T(8,128)(2,1)} %copy.81), calls=%async_computation.6 | async-start | bytes 1048576 | tf_op jit(solution)/shard_map/all_to_all | solution.py:112
  93.6 8.5 %fusion.26 = bf16[512,4,128]{0,2,1:T(8,128)(2,1)} fusion(bf16[512,4,128]{0,2,1:T(8,128)(2,1)S(1)} %copy.75, f32[4,512,512]{1,2,0:T(8,128)} %fusion.54, f32[4,512,512]{1,2,0:T(8,128)} %get-tuple-element.94, f32[4,512]{1,0:T(4,128)S(1)} %get-tuple-element.93), kind=kOutput, calls=%fused_computation.31 | convolution fusion | flops 276040192 | bytes 9445376 | tf_op jit(solution)/shard_map/while/body/eval_jaxpr/hst,thd->shd/dot_general | solution.py:74
  102.1 1.2 convert_element_type.103
  103.3 0.9 copy.77
  104.2 0.0 all-to-all-done.6
  104.2 4.3 %all-to-all-start.5 = ((bf16[4,128,512]{1,2,0:T(8,128)(2,1)}), bf16[4,128,512]{1,2,0:T(8,128)(2,1)}, u32[]{:S(2)}, u32[]{:S(2)}) async-start(bf16[4,128,512]{1,2,0:T(8,128)(2,1)} %copy.77), calls=%async_computation.5 | async-start | bytes 1048576 | tf_op jit(solution)/shard_map/all_to_all | solution.py:111
  108.5 0.3 copy.85
  108.8 1.0 copy.89
  109.8 0.3 copy.71
  110.0 0.0 copy-start
  110.1 0.0 copy-start.4
  110.1 1.0 copy.88
  111.1 0.1 convert_element_type.121
  111.2 0.3 copy.82
  111.5 5.8 %all-to-all-done.5 = bf16[4,128,512]{1,2,0:T(8,128)(2,1)} async-done(((bf16[4,128,512]{1,2,0:T(8,128)(2,1)}), bf16[4,128,512]{1,2,0:T(8,128)(2,1)}, u32[]{:S(2)}, u32[]{:S(2)}) %all-to-all-start.5) | async-done | bytes 524320 | tf_op jit(solution)/shard_map/all_to_all | solution.py:111
  117.3 2.1 %convert_element_type.120 = f32[4,128,512]{1,2,0:T(8,128)} convert(bf16[4,128,512]{1,2,0:T(8,128)(2,1)} %all-to-all-done.5) | non-fusion elementwise | flops 262144 | bytes 1572864 | tf_op jit(solution)/shard_map/convert_element_type | solution.py:18
  119.4 1.6 copy.78
  121.0 0.6 fusion.39
  121.7 38.0 %all-reduce = (f32[2048]{0:T(1024)S(1)}, f32[2048]{0:T(1024)S(1)}) all-reduce(f32[2048]{0:T(1024)S(1)} %get-tuple-element.71, f32[2048]{0:T(1024)S(1)} %get-tuple-element.96), channel_id=1, replica_groups=mesh['dp'=8,'seq'=4] {'dp'}, use_global_device_ids=true, to_apply=%region_8.9 | all-reduce | flops 4096 | bytes 32768 | tf_op jit(solution)/shard_map/psum | solution.py:118
  159.7 10.7 %all-reduce.1 = (f32[2048]{0:T(1024)}, f32[2048]{0:T(1024)}) all-reduce(f32[2048]{0:T(1024)S(1)} %get-tuple-element.85, f32[2048]{0:T(1024)S(1)} %get-tuple-element.86), channel_id=1, replica_groups=mesh['dp'=8,'seq'=4] {'seq'}, use_global_device_ids=true, to_apply=%region_9.10 | all-reduce | flops 4096 | bytes 32768 | tf_op jit(solution)/shard_map/psum | solution.py:117
  170.4 1.2 fusion.36
  171.6 1.2 fusion.45
  (15 shorter events, 0.1 us)
Async XLA Ops:
  0.6 9.0 %copy-start.1 = (bf16[128,2048]{1,0:T(8,128)(2,1)S(1)}, bf16[128,2048]{1,0:T(8,128)(2,1)}, u32[]{:S(2)}) copy-start(bf16[128,2048]{1,0:T(8,128)(2,1)} %param.9) | copy-start | bytes 1572868
  0.6 9.0 %copy-start.5 = (f32[2048]{0:T(1024)S(1)}, f32[2048]{0:T(1024)}, u32[]{:S(2)}) copy-start(f32[2048]{0:T(1024)} %param.12) | copy-start | bytes 24580
  0.7 20.0 %copy-start.2 = (bf16[128,2048]{1,0:T(8,128)(2,1)S(1)}, bf16[128,2048]{1,0:T(8,128)(2,1)}, u32[]{:S(2)}) copy-start(bf16[128,2048]{1,0:T(8,128)(2,1)} %param.10) | copy-start | bytes 1572868
  3.2 29.7 %copy-start.3 = (bf16[128,2048]{1,0:T(8,128)(2,1)S(1)}, bf16[128,2048]{1,0:T(8,128)(2,1)}, u32[]{:S(2)}) copy-start(bf16[128,2048]{1,0:T(8,128)(2,1)} %param.13) | copy-start | bytes 1572868
  4.1 13.1 %all-to-all-start = ((bf16[128,4,512]{2,0,1:T(8,128)(2,1)}), bf16[128,4,512]{2,0,1:T(8,128)(2,1)S(1)}, u32[]{:S(2)}, u32[]{:S(2)}) async-start(bf16[128,4,512]{2,0,1:T(8,128)(2,1)} %bitcast.48), calls=%async_computation | async-start | bytes 1048576 | tf_op jit(solution)/shard_map/all_to_all | solution.py:100
  8.3 36.8 %copy-start.7 = (s32[1,512]{1,0:T(1,128)S(1)}, s32[1,512]{1,0:T(1,128)}, u32[]{:S(2)}) copy-start(s32[1,512]{1,0:T(1,128)} %param.15) | copy-start | bytes 6148
  8.3 36.8 %copy-start.6 = (s32[1,512]{1,0:T(1,128)S(1)}, s32[1,512]{1,0:T(1,128)}, u32[]{:S(2)}) copy-start(s32[1,512]{1,0:T(1,128)} %param.14) | copy-start | bytes 6148
  17.2 12.3 %all-to-all-start.1 = ((bf16[128,4,512]{2,0,1:T(8,128)(2,1)}), bf16[128,4,512]{2,0,1:T(8,128)(2,1)S(1)}, u32[]{:S(2)}, u32[]{:S(2)}) async-start(bf16[128,4,512]{2,0,1:T(8,128)(2,1)} %bitcast.47), calls=%async_computation.1 | async-start | bytes 1048576 | tf_op jit(solution)/shard_map/all_to_all | solution.py:101
  29.4 12.3 %all-to-all-start.2 = ((bf16[128,4,512]{2,0,1:T(8,128)(2,1)}), bf16[128,4,512]{2,0,1:T(8,128)(2,1)S(1)}, u32[]{:S(2)}, u32[]{:S(2)}) async-start(bf16[128,4,512]{2,0,1:T(8,128)(2,1)} %bitcast.46), calls=%async_computation.2 | async-start | bytes 1048576 | tf_op jit(solution)/shard_map/all_to_all | solution.py:102
  41.7 12.3 %all-to-all-start.4 = ((bf16[128,4,512]{2,0,1:T(8,128)(2,1)}), bf16[128,4,512]{2,0,1:T(8,128)(2,1)S(1)}, u32[]{:S(2)}, u32[]{:S(2)}) async-start(bf16[128,4,512]{2,0,1:T(8,128)(2,1)} %bitcast.45), calls=%async_computation.4 | async-start | bytes 1048576 | tf_op jit(solution)/shard_map/all_to_all | solution.py:106
  63.1 12.3 %all-to-all-start.7 = ((bf16[4,128,512]{2,1,0:T(8,128)(2,1)}), bf16[4,128,512]{2,1,0:T(8,128)(2,1)S(1)}, u32[]{:S(2)}, u32[]{:S(2)}) async-start(bf16[4,128,512]{2,1,0:T(8,128)(2,1)} %convert_element_type.117), calls=%async_computation.7 | async-start | bytes 1048576 | tf_op jit(solution)/shard_map/all_to_all | solution.py:113
  75.3 14.8 %all-to-all-start.3 = ((bf16[4,128,512]{2,1,0:T(8,128)(2,1)}), bf16[4,128,512]{2,1,0:T(8,128)(2,1)S(1)}, u32[]{:S(2)}, u32[]{:S(2)}) async-start(bf16[4,128,512]{2,1,0:T(8,128)(2,1)} %convert_element_type.99), calls=%async_computation.3 | async-start | bytes 1048576 | tf_op jit(solution)/shard_map/all_to_all | solution.py:105
  90.1 14.0 %all-to-all-start.6 = ((bf16[4,128,512]{1,2,0:T(8,128)(2,1)}), bf16[4,128,512]{1,2,0:T(8,128)(2,1)S(1)}, u32[]{:S(2)}, u32[]{:S(2)}) async-start(bf16[4,128,512]{1,2,0:T(8,128)(2,1)} %copy.81), calls=%async_computation.6 | async-start | bytes 1048576 | tf_op jit(solution)/shard_map/all_to_all | solution.py:112
  104.2 13.2 %all-to-all-start.5 = ((bf16[4,128,512]{1,2,0:T(8,128)(2,1)}), bf16[4,128,512]{1,2,0:T(8,128)(2,1)}, u32[]{:S(2)}, u32[]{:S(2)}) async-start(bf16[4,128,512]{1,2,0:T(8,128)(2,1)} %copy.77), calls=%async_computation.5 | async-start | bytes 1048576 | tf_op jit(solution)/shard_map/all_to_all | solution.py:111
  110.0 10.9 %copy-start = (bf16[128,2048]{1,0:T(8,128)(2,1)S(1)}, bf16[128,2048]{1,0:T(8,128)(2,1)}, u32[]{:S(2)}) copy-start(bf16[128,2048]{1,0:T(8,128)(2,1)} %param.8) | copy-start | bytes 1572868
  110.1 10.9 %copy-start.4 = (f32[2048]{0:T(1024)S(1)}, f32[2048]{0:T(1024)}, u32[]{:S(2)}) copy-start(f32[2048]{0:T(1024)} %param.11) | copy-start | bytes 24580
